TPU v7x, 32 devices: a 4x4x1 block of a 4x4x8 slice. The times are simulated.
32 devices in a mesh: rep: 1 (over z), tp: 4 (over y), dp: 8 (over x, core).
Axes of the slice: x: 4, y: 4, z: 1, core: 2. Of those that a mesh axis runs over, the one named last changes fastest.
The devices are a block of a 4x4x8 slice.
Arguments:
- grad_partial: float32 [8, 8, 1024, 2048], P(('rep', 'dp'), None, None, 'tp')
- momentum: float32 [8, 1024, 2048], P('rep', 'dp', 'tp')
- weight: float32 [8, 1024, 2048], P('rep', 'dp', 'tp')
- learn_rate: float32 [8], P('rep')
- decay_rate: float32 [], replicated
Outputs:
- output 1: float32 [8, 1024, 2048], P('rep', 'dp', 'tp')
- output 2: float32 [8, 1024, 2048], P('rep', 'dp', 'tp')
- output 3: bfloat16 [8, 1024, 2048], P('rep', None, 'tp')
All inputs are finite; a program needn't handle non-finite values.
Results may differ from a plain program's by a relative error of at most 0.0131368.
Values are sent between devices in bfloat16 or wider.
A program may use at most 768 MiB of HBM per device.

v0:
```python
import functools
import math

import jax
import jax.numpy as jnp
from jax import lax
from jax.experimental import pallas as pl
from jax.experimental.pallas import tpu as pltpu
from jax.sharding import PartitionSpec as P

MOMENTUM = 0.95
NS_STEPS = 5
COEF_A = 3.4445
COEF_B = -4.7750
COEF_C = 2.0315
NORM_EPS = 1e-7
MESH = pl.DeviceIdType.MESH
F32 = jnp.float32
BF16 = jnp.bfloat16
CHUNKS = 8
SLOTS = 6


def make_plan(waves, stages):
    wire, lat, gather_wire, small = 1.41, 2.0, 2.81, 0.7
    step = (1.4, 1.4, 1.5, 0.05, 1.68, 1.68)
    now, link, ylink = 2.0, 0.0, 0.0
    waiting = []
    fresh = [(w, q) for w in range(waves) for q in range(CHUNKS)]
    rank = {"ring": 0, "gather": 1, "half": 2, "pair": 3}

    def run(event):
        nonlocal now, link, ylink
        kind, w, q = event[:3]
        now += 0.06
        if kind == "ring" and event[3] < stages:
            link = max(link, now) + wire
            waiting.append((link + lat, ("ring", w, q, event[3] + 1)))
        elif kind == "ring":
            link = max(link, now) + small
            waiting.append((link + lat + 0.3, ("gather", w, q)))
        elif kind == "gather":
            ylink = max(ylink, now) + gather_wire
            waiting.append((ylink + lat + 1.5 * w, ("half", w, q)))
        elif kind == "half":
            waiting.append((now + 1.7, ("pair", w, q)))

    def take(limit, late=0.0):
        nonlocal now
        due = [item for item in waiting if item[0] <= limit - late * item[1][1]]
        if not due:
            return None
        best = min(due, key=lambda item: (item[1][1], rank[item[1][0]], item[0]))
        waiting.remove(best)
        now = max(now, best[0])
        return best[1]

    before, slots, after = [], {}, []
    todo = CHUNKS
    while todo:
        event = take(now, 1.5)
        usable, depth = False, 1.2
        if fresh and fresh[0][0]:
            started = len([e for e in before if e[1] and e[0] == "ring" and not e[3]])
            usable = ("ring", 0, CHUNKS - 1, stages - 1) in before and started < 1
            usable = usable or ("ring", 0, CHUNKS - 1, stages) in before
        elif fresh:
            usable = True
        if event is None and usable and link - now < depth:
            event = ("ring", *fresh.pop(0), 0)
        if event is None:
            times = [item[0] + 1.5 * item[1][1] for item in waiting]
            if usable:
                times.append(link - depth + 0.01)
            now = max(now + 0.01, min(times))
            continue
        run(event)
        before.append(event)
        todo -= event[0] == "pair" and event[1] == 0
    clock = now + 1.3
    for it in range(NS_STEPS):
        for slot in range(SLOTS if it < NS_STEPS - 1 else 4):
            clock += step[slot]
            now = clock
            found = []
            while True:
                event = take(now - 0.3)
                if event is None and fresh and link - now < 2.0:
                    event = ("ring", *fresh.pop(0), 0)
                if event is None:
                    break
                run(event)
                found.append(event)
            clock = now
            slots[it, slot] = found
    while fresh or waiting:
        if fresh:
            event = ("ring", *fresh.pop(0), 0)
        else:
            event = take(min(item[0] for item in waiting))
        run(event)
        after.append(event)
    return before, slots, after


def dot_nt(lhs, rhs):
    return lax.dot_general(lhs, rhs, (((1,), (1,)), ((), ())), preferred_element_type=F32)


def dot_nn(lhs, rhs):
    return jnp.dot(lhs, rhs, preferred_element_type=F32)


def muon_kernel(
    dims, grad, mom, wgt, rate, decay, momv, wgtv, full,
    gown, gpar, ring, usend, xs0, xs1, xs2, aown, apar, bmat, xfin, xback, sums,
    own_sem, mw_sem, gp_s, gp_r, ring_s, ring_r, a2a_s, a2a_r, yg_s, yg_r, half_s, half_r,
    xe_s, xe_r, ae_s, ae_r, bk_s, bk_r, ag_s, ag_r, ad_s, ad_r,
):
    nx, tp, mats, rows, cols = dims
    waves = mats // nx
    piece = rows // CHUNKS
    half = nx * rows
    width = tp * cols
    blk = min(256, half // 2)
    nblk = min(256, cols // 2)
    xs = (xs0, xs1)
    pong = xs2
    out_scale = 0.2 * math.sqrt(max(2 * half, width))

    d = lax.axis_index("dp")
    y = lax.axis_index("tp")
    x = d // 2
    c = d % 2
    turn = 1 - 2 * c
    nxt_x = (x + turn + nx) % nx
    partner = {"dp": 2 * x + (1 - c)}
    right = {"dp": 2 * nxt_x + c}

    my_cols = pl.ds(pl.multiple_of(y * cols, cols), cols)

    def at_x(dx):
        return {"dp": 2 * ((x + dx) % nx) + c}

    def at_y(dy):
        return {"tp": (y + dy) % tp}

    def remote(src, dst, send, recv, dev):
        return pltpu.make_async_remote_copy(
            src_ref=src, dst_ref=dst, send_sem=send, recv_sem=recv, device_id=dev, device_id_type=MESH
        )

    def all_of(like, sem):
        pltpu.make_async_copy(like, like, sem).wait()

    def wave(w):
        return pl.ds(w * nx, nx)

    def part(q):
        return pl.ds(q * piece, piece)

    def own_load(w, q):
        return pltpu.make_async_copy(
            grad.at[wave(w), :, c, part(q)], gown.at[wave(w), :, part(q)], own_sem.at[w, q]
        )

    def pair_copy(w, q):
        return remote(
            grad.at[wave(w), :, 1 - c, part(q)], gpar.at[wave(w), :, part(q)], gp_s.at[0], gp_r.at[w, q], partner
        )

    mom_load = pltpu.make_async_copy(mom, momv, mw_sem.at[0])
    wgt_load = pltpu.make_async_copy(wgt, wgtv, mw_sem.at[1])
    for w in range(waves):
        for q in range(CHUNKS):
            own_load(w, q).start()
    mom_load.start()
    wgt_load.start()

    barrier = pltpu.get_barrier_semaphore()
    peers = [partner] + [at_x(dx) for dx in range(1, nx)] + [at_y(dy) for dy in range(1, tp)]
    for peer in peers:
        pl.semaphore_signal(barrier, inc=1, device_id=peer, device_id_type=MESH)
    pl.semaphore_wait(barrier, len(peers))
    for w in range(waves):
        for q in range(CHUNKS):
            pair_copy(w, q).start()

    def ring_block(stage):
        return (x - turn * (1 + stage) + 4 * nx) % nx

    def ring_copy(w, q, stage):
        if stage == 0:
            src = gown.at[wave(w), ring_block(0), part(q)]
        else:
            src = ring.at[w, q, stage - 1]
        return remote(src, ring.at[w, q, stage], ring_s.at[0], ring_r.at[w, q, stage], right)

    def a2a_copy(w, q, dx):
        owner = (x + dx) % nx
        return remote(
            usend.at[w * nx + owner, part(q)],
            xs[w].at[0, x, part(q), my_cols],
            a2a_s.at[0], a2a_r.at[w, q], at_x(dx),
        )

    def ring_event(w, q, stage):
        block = ring_block(stage)
        if stage == 0:
            own_load(w, q).wait()
            pair_copy(w, q).wait_recv()
        else:
            ring_copy(w, q, stage - 1).wait_recv()
        for i in range(nx):
            m = w * nx + i
            local = gown[m, block, part(q)] + gpar[m, block, part(q)]
            if stage == 0:
                gown[m, block, part(q)] = local
            elif stage < nx - 1:
                ring[w, q, stage - 1, i] = ring[w, q, stage - 1, i] + local
            else:
                grad_mean = (ring[w, q, stage - 1, i] + local) * (1.0 / (2 * nx))
                mom_new = MOMENTUM * momv[m, part(q)] + grad_mean
                momv[m, part(q)] = mom_new
                usend[m, part(q)] = (grad_mean + MOMENTUM * mom_new).astype(BF16)
        if stage < nx - 1:
            ring_copy(w, q, stage).start()
        else:
            for dx in (2, 1, 3):
                a2a_copy(w, q, dx).start()
            xs[w][0, x, part(q), my_cols] = usend[w * nx + x, part(q)]

    def gather_copy(w, q, dy):
        region = xs[w].at[0, :, part(q), my_cols]
        return remote(region, region, yg_s.at[w], yg_r.at[w, q], at_y(dy))

    def half_copy(w, q):
        return remote(
            xs[w].at[0, :, part(q)], xs[w].at[1, :, part(q)], half_s.at[w], half_r.at[w, q], partner
        )

    def gather_event(w, q):
        all_of(usend.at[pl.ds(0, nx - 1), part(q)], a2a_r.at[w, q])
        for dy in (2, 1, 3):
            if dy < tp:
                gather_copy(w, q, dy).start()

    def add_squares(w, side, q):
        acc = sums[w]
        for i in range(nx):
            v = xs[w][side, i, part(q), :].astype(F32)
            v = v * v
            for n in range(width // 128):
                acc = acc + v[:, n * 128:(n + 1) * 128]
        sums[w] = acc

    def half_event(w, q):
        all_of(xs[w].at[0, :, part(q), pl.ds(0, width - cols)], yg_r.at[w, q])
        half_copy(w, q).start()
        add_squares(w, 0, q)

    def pair_event(w, q):
        half_copy(w, q).wait_recv()
        add_squares(w, 1, q)

    def normalise(w):
        all_of(xs[w].at[0], half_s.at[w])
        all_of(xs[w].at[0, :, :, pl.ds(0, width - cols)], yg_s.at[w])
        total = jnp.sum(sums[w])
        inv = 1.0 / (jnp.sqrt(jnp.full((8, 128), total, F32)) + NORM_EPS)
        inv = inv[0:1, 0:1]

        def scale_rows(r, carry):
            sl = pl.ds(pl.multiple_of(r * 16, 16), 16)
            for side in range(2):
                for i in range(nx):
                    xs[w][side, i, sl, :] = (xs[w][side, i, sl, :].astype(F32) * inv).astype(BF16)
            return carry

        lax.fori_loop(0, rows // 16, scale_rows, 0)

    own = pl.ds(0, half)
    own_blocks = half // blk
    n_chunks = width // nblk
    batch = max(1, n_chunks // 2)

    def chunk_copy(dst, par, n):
        col = pl.ds(pl.multiple_of(n * nblk, nblk), nblk)
        return remote(dst.at[0, :, :, col], dst.at[1, :, :, col], xe_s.at[par], xe_r.at[par], partner)

    def newton_schulz(w, service):
        def a_copy(par):
            slot = (par + w) % 2
            return remote(aown.at[:, own], apar.at[slot], ae_s.at[slot], ae_r.at[slot], partner)

        def a_block(cur, side, j):
            per = blk // rows if blk >= rows else 1
            rhs = cur[side, j * per:(j + 1) * per].reshape(blk, width)
            lhs = cur[0].reshape(half, width)
            col = (side * own_blocks + j) * blk
            aown[:, col:col + blk] = dot_nt(lhs, rhs).astype(BF16)

        def b_own(j):
            rs = slice(j * blk, (j + 1) * blk)
            sq = dot_nt(aown[...], aown[rs, :])
            bmat[:, rs] = (COEF_B * aown[:, rs].astype(F32) + COEF_C * sq).astype(BF16)

        def b_other(par, j):
            rs = slice(j * blk, (j + 1) * blk)
            ps = slice(half + j * blk, half + (j + 1) * blk)
            sq = dot_nn(aown[:, :half], aown[:, ps]) + dot_nn(aown[:, half:], apar[(par + w) % 2, :, rs])
            bmat[:, ps] = (COEF_B * aown[:, ps].astype(F32) + COEF_C * sq).astype(BF16)

        def x_cols(cur, col):
            rhs = cur[:, :, :, col].reshape(2 * half, nblk)
            new = COEF_A * cur[0, :, :, col].reshape(half, nblk).astype(F32) + dot_nn(bmat[...], rhs)
            return new.astype(BF16)

        def iteration(it, par, cur, nxt, first, final):
            def drain_a():
                a_copy(1 - par).wait_send()

            def need_x():
                all_of(cur.at[0], xe_s.at[1 - par])
                all_of(cur.at[1], xe_r.at[1 - par])

            def guarded(fn):
                if first is False:
                    fn()
                else:
                    pl.when(jnp.logical_not(first))(fn)

            guarded(drain_a)
            for j in range(own_blocks):
                a_block(cur, 0, j)
            a_copy(par).start()
            service(it, 0)
            guarded(need_x)
            for j in range(own_blocks):
                a_block(cur, 1, j)
            service(it, 1)
            a_copy(par).wait_recv()
            for j in range(own_blocks):
                b_own(j)
            for j in range(own_blocks):
                b_other(par, j)
            service(it, 2)
            service(it, 3)
            if final:
                for n in range(cols // nblk):
                    col = pl.ds(pl.multiple_of(y * cols + n * nblk, nblk), nblk)
                    xfin[w, :, :, n * nblk:(n + 1) * nblk] = x_cols(cur, col).reshape(nx, rows, nblk)
            else:
                def x_pair(k, carry):
                    cols_of = [pl.ds(pl.multiple_of((2 * k + e) * nblk, nblk), nblk) for e in range(2)]
                    for col in cols_of:
                        nxt[0, :, :, col] = x_cols(cur, col).reshape(nx, rows, nblk)
                    for e in range(2):
                        chunk_copy(nxt, par, 2 * k + e).start()
                    return carry

                for part_no in range(2):
                    lax.fori_loop(part_no * batch // 2, (part_no + 1) * batch // 2, x_pair, 0)
                    service(it, 4 + part_no)

        def pair_of_steps(p, carry):
            iteration((p, 0), 0, xs[w], pong, p == 0, False)
            iteration((p, 1), 1, pong, xs[w], False, False)
            return carry

        lax.fori_loop(0, NS_STEPS // 2, pair_of_steps, 0)
        iteration(NS_STEPS - 1, 0, xs[w], None, False, True)
        a_copy(0).wait_send()

    def back_copy(w, dx):
        return remote(
            xfin.at[w, (x + dx) % nx],
            xback.at[w * nx + x], bk_s.at[0], bk_r.at[w, dx], at_x(dx),
        )

    def back_arrival(w, dx):
        m = w * nx + (x - dx + nx) % nx
        return remote(
            xfin.at[w, 0], xback.at[m], bk_s.at[0], bk_r.at[w, dx], at_x(dx)
        )

    def back_send(w):
        for dx in (2, 1, 3):
            back_copy(w, dx).start()
        xback[w * nx + x] = xfin[w, x]

    order = (0, 1, 3, 2)

    def gather_slot(w, hop, j):
        holder = (x - turn * hop + 4 * nx) % nx
        return holder, w * nx + (holder - order[j] + nx) % nx

    def ag_copy(w, hop, j):
        holder, m = gather_slot(w, hop, j)
        block = full.at[m, holder, c]
        return remote(block, block, ag_s.at[0], ag_r.at[m, hop], right)

    def ag_arrival(w, hop, j):
        holder, m = gather_slot(w, hop + 1, j)
        block = full.at[m, holder, c]
        return remote(block, block, ag_s.at[0], ag_r.at[m, hop], right)

    def pair_full(w, hop, j):
        holder, m = gather_slot(w, hop, j)
        block = full.at[m, holder, c]
        return remote(block, block, ad_s.at[0], ad_r.at[w], partner)

    def weight_event(w, j):
        dx = order[j]
        m = w * nx + (x - dx + nx) % nx
        if dx:
            back_arrival(w, dx).wait_recv()
        w_old = wgtv[m]
        w_new = w_old - rate[m] * (out_scale * xback[m].astype(F32) + decay[0] * w_old)
        wgtv[m] = w_new
        full[m, x, c] = w_new.astype(BF16)
        ag_copy(w, 0, j).start()
        pair_full(w, 0, j).start()

    def forward_event(w, hop, j):
        ag_arrival(w, hop - 1, j).wait_recv()
        if hop < nx - 1:
            ag_copy(w, hop, j).start()
        pair_full(w, hop, j).start()

    def finish_gather(w):
        all_of(full.at[wave(w), :, 1 - c], ad_r.at[w])

    handlers = {"ring": ring_event, "gather": gather_event, "half": half_event, "pair": pair_event}

    def perform(events):
        for kind, *rest in events:
            handlers[kind](*rest)

    def server(table):
        def service(it, slot):
            if isinstance(it, tuple):
                p, odd = it
                for k in range(NS_STEPS // 2):
                    work = table.get((2 * k + odd, slot), [])
                    if work:
                        pl.when(p == k)(functools.partial(perform, work))
            else:
                perform(table.get((it, slot), []))
        return service

    handlers["weight"] = weight_event
    handlers["forward"] = forward_event
    before, during, after = make_plan(waves, nx - 1)
    for w in range(waves):
        sums[w] = jnp.zeros((piece, 128), F32)
    mom_load.wait()
    perform(before)
    normalise(0)
    newton_schulz(0, server(during))
    back_send(0)
    wgt_load.wait()
    perform([e for e in after if e[0] in ("ring", "gather")])
    perform([("weight", 0, 0)])
    perform([e for e in after if e[0] in ("half", "pair")])
    normalise(1)
    second = {
        (0, 4): [("weight", 0, 1)], (0, 5): [("weight", 0, 2)], (1, 0): [("weight", 0, 3)],
        (1, 2): [("forward", 0, 1, 0)], (1, 3): [("forward", 0, 1, 1)],
        (1, 4): [("forward", 0, 1, 2)], (1, 5): [("forward", 0, 1, 3)],
        (2, 2): [("forward", 0, 2, 0)], (2, 3): [("forward", 0, 2, 1)],
        (2, 4): [("forward", 0, 2, 2)], (2, 5): [("forward", 0, 2, 3)],
        (3, 2): [("forward", 0, 3, 0)], (3, 3): [("forward", 0, 3, 1)],
        (3, 4): [("forward", 0, 3, 2)], (3, 5): [("forward", 0, 3, 3)],
    }
    newton_schulz(1, server(second))
    back_send(1)
    perform([("weight", 1, j) for j in range(nx)])
    perform([("forward", 1, hop, j) for hop in range(1, nx) for j in range(nx)])
    for w in range(waves):
        finish_gather(w)

    all_of(gpar, gp_s.at[0])
    all_of(ring, ring_s.at[0])
    all_of(usend.at[pl.ds(0, waves * (nx - 1))], a2a_s.at[0])
    all_of(xback.at[pl.ds(0, waves * (nx - 1))], bk_s.at[0])
    all_of(full.at[:, pl.ds(0, nx - 1), 0], ag_s.at[0])
    all_of(full.at[:, :, 0], ad_s.at[0])


def store_kernel(a, b, c, a_out, b_out, c_out, sem):
    cut = a.shape[0] // 2
    pieces = [(c.at[m], c_out.at[m]) for m in range(c.shape[0])]
    for src, dst in ((a, a_out), (b, b_out)):
        pieces += [(src.at[pl.ds(k * cut, cut)], dst.at[pl.ds(k * cut, cut)]) for k in range(2)]
    copies = [pltpu.make_async_copy(src, dst, sem.at[i]) for i, (src, dst) in enumerate(pieces)]
    for copy in copies:
        copy.start()
    for copy in copies:
        copy.wait()


def solution(mesh):
    dp = mesh.shape["dp"]
    tp = mesh.shape["tp"]
    nx = dp // 2

    def local_step(grad_local, mom_local, weight_local, learn_rate, decay_rate):
        mats, rows, cols = mom_local.shape
        waves = mats // nx
        piece = rows // CHUNKS
        half = nx * rows
        width = tp * cols
        n_chunks = width // min(256, cols // 2)
        dma = pltpu.SemaphoreType.DMA
        vmem = pltpu.VMEM
        anyspec = pl.BlockSpec(memory_space=pl.ANY)
        smem = pl.BlockSpec(memory_space=pltpu.SMEM)
        vspec = pl.BlockSpec(memory_space=pltpu.VMEM)
        grad_view = grad_local.reshape(mats, nx, 2, rows, cols)
        call = pl.pallas_call(
            functools.partial(muon_kernel, (nx, tp, mats, rows, cols)),
            out_shape=(
                vmem((mats, rows, cols), F32),
                vmem((mats, rows, cols), F32),
                vmem((mats, nx, 2, rows, cols), BF16),
            ),
            in_specs=[anyspec, anyspec, anyspec, smem, smem],
            out_specs=(vspec, vspec, vspec),
            scratch_shapes=[
                vmem((mats, nx, rows, cols), F32),
                vmem((mats, nx, rows, cols), F32),
                vmem((waves, CHUNKS, nx - 1, nx, piece, cols), F32),
                vmem((mats, rows, cols), BF16),
                vmem((2, nx, rows, width), BF16),
                vmem((2, nx, rows, width), BF16),
                vmem((2, nx, rows, width), BF16),
                vmem((half, 2 * half), BF16),
                vmem((2, half, half), BF16),
                vmem((half, 2 * half), BF16),
                vmem((waves, nx, rows, cols), BF16),
                vmem((mats, rows, cols), BF16),
                vmem((waves, piece, 128), F32),
                dma((waves, CHUNKS)),
                dma((2,)),
                dma((1,)),
                dma((waves, CHUNKS)),
                dma((1,)),
                dma((waves, CHUNKS, nx - 1)),
                dma((1,)),
                dma((waves, CHUNKS)),
                dma((waves,)),
                dma((waves, CHUNKS)),
                dma((waves,)),
                dma((waves, CHUNKS)),
                dma((2,)),
                dma((2,)),
                dma((2,)),
                dma((2,)),
                dma((1,)),
                dma((waves, nx)),
                dma((1,)),
                dma((mats, nx - 1)),
                dma((1,)),
                dma((waves,)),
            ],
            compiler_params=pltpu.CompilerParams(
                collective_id=0, has_side_effects=True, vmem_limit_bytes=46 * 1024 * 1024
            ),
        )
        results = call(grad_view, mom_local, weight_local, learn_rate, decay_rate.reshape(1))
        results = [pltpu.with_memory_space_constraint(r, pltpu.VMEM) for r in results]
        mom_new, weight_new, full = pl.pallas_call(
            store_kernel,
            out_shape=tuple(jax.ShapeDtypeStruct(r.shape, r.dtype) for r in results),
            in_specs=[vspec] * 3,
            out_specs=(anyspec,) * 3,
            scratch_shapes=[dma((mats + 4,))],
            compiler_params=pltpu.CompilerParams(vmem_limit_bytes=1024 * 1024),
        )(*results)
        return mom_new, weight_new, full.reshape(mats, dp * rows, cols)

    return jax.shard_map(
        local_step,
        mesh=mesh,
        in_specs=(P(("rep", "dp"), None, None, "tp"), P("rep", "dp", "tp"), P("rep", "dp", "tp"), P("rep"), P()),
        out_specs=(P("rep", "dp", "tp"), P("rep", "dp", "tp"), P("rep", None, "tp")),
        check_vma=False,
    )
```

profile of v0, /device:TPU:97, one launch (start us, length us, event | category | flops | bytes accessed | tf_op | source)
XLA Modules:
  0.0 177.6 jit_solution(11693246486628357458)
XLA Ops:
  1.3 171.4 %shard_map.76 = (f32[8,128,512]{2,1,0:T(8,128)S(1)}, f32[8,128,512]{2,1,0:T(8,128)S(1)}, bf16[8,4,2,128,512]{4,3,2,1,0:T(8,128)(2,1)S(1)}) custom-call(f32[8,4,2,128,512]{4,3,2,1,0:T(8,128)} %bitcast.4, f32[8,128,512]{2,1,0:T(8,128)} %mom.1, f32[8,128,512]{2,1,0:T(8,128)} %wgt.1, f32[8]{0:T(128)} %rate.1, f32[1]{0:T(128)} %bitcast.3.decay), custom_call_target="tpu_custom_call" | custom-call | tf_op jit(solution)/shard_map/pallas_call | solution.py:571
  172.7 4.7 %shard_map.77 = (f32[8,128,512]{2,1,0:T(8,128)}, f32[8,128,512]{2,1,0:T(8,128)}, bf16[8,4,2,128,512]{4,3,2,1,0:T(8,128)(2,1)}) custom-call(f32[8,128,512]{2,1,0:T(8,128)S(1)} %get-tuple-element.9.a, f32[8,128,512]{2,1,0:T(8,128)S(1)} %get-tuple-element.10.b, bf16[8,4,2,128,512]{4,3,2,1,0:T(8,128)(2,1)S(1)} %get-tuple-element.11.c), custom_call_target="tpu_custom_call" | custom-call | tf_op jit(solution)/shard_map/pallas_call | solution.py:573
where the time goes:
time: 178 us
  Pallas kernels  176 us (99%)
    pallas_call x1, Pallas kernels, local_step(): call(grad_view, mom_local, weight_local, learn_rate, decay_rate.reshape(1))  171 us
    pallas_call x1, Pallas kernels, local_step(): pl.pallas_call(store_kernel, out_shape=tuple((jax.ShapeDtypeStruct(r.shap...  4.67 us

commit v1 on v0

--- a/solution.py
+++ b/solution.py
@@ -22,7 +22,7 @@
 
 
 def make_plan(waves, stages):
-    wire, lat, gather_wire, small = 1.41, 2.0, 2.81, 0.7
+    wire, lat, gather_wire, small = 1.41, 2.4, 2.81, 0.7
     step = (1.4, 1.4, 1.5, 0.05, 1.68, 1.68)
     now, link, ylink = 2.0, 0.0, 0.0
     waiting = []
@@ -59,11 +59,10 @@
     todo = CHUNKS
     while todo:
         event = take(now, 1.5)
-        usable, depth = False, 1.2
+        usable, depth = False, 2.0
         if fresh and fresh[0][0]:
             started = len([e for e in before if e[1] and e[0] == "ring" and not e[3]])
-            usable = ("ring", 0, CHUNKS - 1, stages - 1) in before and started < 1
-            usable = usable or ("ring", 0, CHUNKS - 1, stages) in before
+            usable = ("ring", 0, CHUNKS - 1, stages) in before and started < 4
         elif fresh:
             usable = True
         if event is None and usable and link - now < depth:
@@ -77,15 +76,15 @@
         run(event)
         before.append(event)
         todo -= event[0] == "pair" and event[1] == 0
-    clock = now + 1.3
+    clock, lat = now + 1.3, 2.1
     for it in range(NS_STEPS):
         for slot in range(SLOTS if it < NS_STEPS - 1 else 4):
             clock += step[slot]
             now = clock
             found = []
             while True:
-                event = take(now - 0.3)
-                if event is None and fresh and link - now < 2.0:
+                event = take(now - 0.1)
+                if event is None and fresh and link - now < 2.5:
                     event = ("ring", *fresh.pop(0), 0)
                 if event is None:
                     break
@@ -385,7 +384,7 @@
         )
 
     def back_send(w):
-        for dx in (2, 1, 3):
+        for dx in (1, 3, 2):
             back_copy(w, dx).start()
         xback[w * nx + x] = xfin[w, x]
 

time: 178 us -> 180 us (1.011)
  Pallas kernels: 176 us -> 178 us
    pallas_call x1, Pallas kernels: 171 us -> 174 us  [local_step(): call(grad_view, mom_local, weight_local, learn_rate, decay_rate.reshape(1))]
where the time goes in v1:
time: 180 us
  Pallas kernels  178 us (99%)
    pallas_call x1, Pallas kernels, local_step(): call(grad_view, mom_local, weight_local, learn_rate, decay_rate.reshape(1))  174 us
    pallas_call x1, Pallas kernels, local_step(): pl.pallas_call(store_kernel, out_shape=tuple((jax.ShapeDtypeStruct(r.shap...  4.67 us

profile of v1, /device:TPU:97, one launch (start us, length us, event | category | flops | bytes accessed | tf_op | source)
XLA Modules:
  0.0 179.7 jit_solution(10941825550198330594)
XLA Ops:
  1.3 173.6 %shard_map.76 = (f32[8,128,512]{2,1,0:T(8,128)S(1)}, f32[8,128,512]{2,1,0:T(8,128)S(1)}, bf16[8,4,2,128,512]{4,3,2,1,0:T(8,128)(2,1)S(1)}) custom-call(f32[8,4,2,128,512]{4,3,2,1,0:T(8,128)} %bitcast.4, f32[8,128,512]{2,1,0:T(8,128)} %mom.1, f32[8,128,512]{2,1,0:T(8,128)} %wgt.1, f32[8]{0:T(128)} %rate.1, f32[1]{0:T(128)} %bitcast.3.decay), custom_call_target="tpu_custom_call" | custom-call | tf_op jit(solution)/shard_map/pallas_call | solution.py:570
  174.9 4.7 %shard_map.77 = (f32[8,128,512]{2,1,0:T(8,128)}, f32[8,128,512]{2,1,0:T(8,128)}, bf16[8,4,2,128,512]{4,3,2,1,0:T(8,128)(2,1)}) custom-call(f32[8,128,512]{2,1,0:T(8,128)S(1)} %get-tuple-element.9.a, f32[8,128,512]{2,1,0:T(8,128)S(1)} %get-tuple-element.10.b, bf16[8,4,2,128,512]{4,3,2,1,0:T(8,128)(2,1)S(1)} %get-tuple-element.11.c), custom_call_target="tpu_custom_call" | custom-call | tf_op jit(solution)/shard_map/pallas_call | solution.py:572

commit v2 on v0

--- a/solution.py
+++ b/solution.py
@@ -385,7 +385,7 @@
         )
 
     def back_send(w):
-        for dx in (2, 1, 3):
+        for dx in (1, 3, 2):
             back_copy(w, dx).start()
         xback[w * nx + x] = xfin[w, x]
 

time: 178 us -> 178 us (level)
  no operation moved by 1% of the time
where the time goes in v2:
time: 178 us
  Pallas kernels  177 us (99%)
    pallas_call x1, Pallas kernels, local_step(): call(grad_view, mom_local, weight_local, learn_rate, decay_rate.reshape(1))  172 us
    pallas_call x1, Pallas kernels, local_step(): pl.pallas_call(store_kernel, out_shape=tuple((jax.ShapeDtypeStruct(r.shap...  4.67 us

profile of v2, /device:TPU:97, one launch (start us, length us, event | category | flops | bytes accessed | tf_op | source)
XLA Modules:
  0.0 178.2 jit_solution(7859359386914352362)
XLA Ops:
  1.3 172.1 %shard_map.76 = (f32[8,128,512]{2,1,0:T(8,128)S(1)}, f32[8,128,512]{2,1,0:T(8,128)S(1)}, bf16[8,4,2,128,512]{4,3,2,1,0:T(8,128)(2,1)S(1)}) custom-call(f32[8,4,2,128,512]{4,3,2,1,0:T(8,128)} %bitcast.4, f32[8,128,512]{2,1,0:T(8,128)} %mom.1, f32[8,128,512]{2,1,0:T(8,128)} %wgt.1, f32[8]{0:T(128)} %rate.1, f32[1]{0:T(128)} %bitcast.3.decay), custom_call_target="tpu_custom_call" | custom-call | tf_op jit(solution)/shard_map/pallas_call | solution.py:571
  173.3 4.7 %shard_map.77 = (f32[8,128,512]{2,1,0:T(8,128)}, f32[8,128,512]{2,1,0:T(8,128)}, bf16[8,4,2,128,512]{4,3,2,1,0:T(8,128)(2,1)}) custom-call(f32[8,128,512]{2,1,0:T(8,128)S(1)} %get-tuple-element.9.a, f32[8,128,512]{2,1,0:T(8,128)S(1)} %get-tuple-element.10.b, bf16[8,4,2,128,512]{4,3,2,1,0:T(8,128)(2,1)S(1)} %get-tuple-element.11.c), custom_call_target="tpu_custom_call" | custom-call | tf_op jit(solution)/shard_map/pallas_call | solution.py:573
